TPU v7x, 32 devices: a whole 2x2x4 slice. The times are simulated.
32 devices in a mesh: tm: 8 (over y, x, core), row: 4 (over z).
Axes of the slice: x: 2, y: 2, z: 4, core: 2. Of those that a mesh axis runs over, the one named last changes fastest.
Arguments:
- starts: float32 [8, 8, 16384], P('tm', None, 'row'), may hold values from -6 to 6
- operator: float32 [16384, 16384], P('row', 'tm'), may hold values from -0.5 to 0.5
- coarse_left: float32 [16384, 256], P('row'), may hold values from -0.375 to 0.375
- coarse_right: float32 [16384, 256], P('row'), may hold values from -0.046875 to 0.046875
Outputs:
- new_ends: float32 [8, 8, 16384], P('tm', None, 'row')
All inputs are finite; a program needn't handle non-finite values.
Results may differ from a plain program's by a relative error of at most 0.00019.
Values sent between devices are 32-bit elements; how exact they have to be, the bound alone decides.
A program may use at most 128 MiB of HBM per device.

v0:
```python
import jax
import jax.numpy as jnp
from jax import lax
from jax.sharding import PartitionSpec as P

FINE = 4


highest = lax.Precision.HIGHEST


def broadcast(array, axis, root):
    mine = lax.axis_index(axis) == root
    return lax.psum(jnp.where(mine, array, jnp.zeros_like(array)), axis)


def carried_in(array, axis, combine, identity):
    peers, place = (lax.axis_size(axis), lax.axis_index(axis))
    everything = lax.all_gather(array, axis)
    start = jnp.broadcast_to(jnp.asarray(identity, array.dtype), array.shape)

    def hop(k, before):
        reached = k < place
        new = combine(before, everything[k])
        return jnp.where(reached, new, before)

    return lax.fori_loop(0, peers, hop, start)


def shifted(block, axis, distance):
    devices = range(lax.axis_size(axis))
    route = [(i - distance, i) for i in devices if i - distance in devices]
    return lax.ppermute(block, axis, route)


def project_rows(values, factor):
    return jnp.einsum("sen,nr->ser", values, factor, precision=highest)


def spread_rows(weights, factor):
    return jnp.einsum("ser,nr->sen", weights, factor, precision=highest)


def matmul(left_side, right_side):
    return jnp.dot(left_side, right_side, precision=highest, preferred_element_type=jnp.float32)


def times_columns(vectors, operator):
    return lax.dot_general(
        vectors,
        operator,
        (((1,), (1,)), ((), ())),
        precision=highest,
        preferred_element_type=jnp.float32,
    )


def walk_slices(zeta_run, total_run, kernel, defect_terms):
    total_run = total_run + zeta_run
    zeta_run = matmul(zeta_run, kernel) + defect_terms[0]
    records = [total_run]
    return (zeta_run, total_run, jnp.stack(records))


def local(starts, operator, coarse_left, coarse_right):
    local_slices = starts.shape[0]
    ensemble = starts.shape[1]
    rows_here = starts.shape[2]
    rank_width = coarse_right.shape[1]
    tm_count = lax.axis_size("tm")
    position = lax.axis_index("tm")
    step_time = 1.0 / (local_slices * tm_count)
    fine_time = step_time / FINE
    flattened = starts.reshape(local_slices * ensemble, rows_here)

    def fine_scatter(done_steps, current):
        full_state = lax.all_gather(current, "row", axis=1, tiled=True)
        columns = lax.all_to_all(full_state, "tm", split_axis=1, concat_axis=0, tiled=True)
        images = lax.psum_scatter(
            times_columns(columns, operator), "tm", scatter_dimension=0, tiled=True
        )
        return current + fine_time * images

    fine_flat = lax.fori_loop(0, FINE, fine_scatter, flattened)
    fine_ends = fine_flat.reshape(local_slices, ensemble, rows_here)
    old_projection = lax.psum(project_rows(starts, coarse_right), "row")
    defects = fine_ends - (starts + step_time * spread_rows(old_projection, coarse_left))
    first_start = broadcast(starts[0], "tm", 0)
    defect_terms, cross_terms, first_terms = lax.psum(
        (
            project_rows(defects, coarse_right),
            matmul(coarse_left.T, coarse_right),
            matmul(first_start, coarse_right),
        ),
        "row",
    )
    kernel = jnp.eye(rank_width, dtype=jnp.float32) + step_time * cross_terms
    running = jnp.cumsum(defects, axis=0)
    before = carried_in(running[-1], "tm", jnp.add, jnp.zeros_like(running[-1]))

    def reduced_turn(turn_index, carried):
        passing, totals = carried
        zeta_run, total_run, records = walk_slices(passing[0], passing[1], kernel, defect_terms)
        active = position == turn_index
        totals = jnp.where(active, records, totals)
        outgoing = jnp.where(active, jnp.stack([zeta_run, total_run]), passing)
        return (shifted(outgoing, "tm", 1), totals)

    entering = jnp.stack([first_terms, jnp.zeros_like(first_terms)])
    projected_sums = lax.fori_loop(
        0, tm_count, reduced_turn, (entering, jnp.zeros_like(defect_terms))
    )[1]
    new_ends = (
        first_start[None]
        + step_time * spread_rows(projected_sums, coarse_left)
        + before[None]
        + running
    )
    return new_ends


def solution(mesh):
    in_specs = (P("tm", None, "row"), P("row", "tm"), P("row", None), P("row", None))
    out_specs = P("tm", None, "row")
    return jax.shard_map(local, mesh=mesh, in_specs=in_specs, out_specs=out_specs, check_vma=False)
```

profile of v0, /device:TPU:0, one launch (start us, length us, event | category | flops | bytes accessed | tf_op | source)
XLA Modules:
  0.0 596.0 jit_solution(946829281519255952)
XLA Ops:
  9.8 406.4 %while.40 = (s32[]{:T(128)}, f32[8,4096]{1,0:T(8,128)S(1)}, f32[4096,2048]{1,0:T(8,128)}, s32[]{:T(128)}) while((s32[]{:T(128)}, f32[8,4096]{1,0:T(8,128)S(1)}, f32[4096,2048]{1,0:T(8,128)}, s32[]{:T(128)}) %tuple.75), condition=%wide.region_5.6_spmd, body=%wide.region_3.5_spmd.sunk | while | flops 6442516480 | bytes 40763484 | solution.py:84
  9.8 17.4 %all_gather.8 = f32[8,16384]{1,0:T(8,128)S(1)} all-gather(f32[8,4096]{1,0:T(8,128)S(1)} %get-tuple-element.369), channel_id=1, replica_groups=mesh['tm'=8,'row'=4] {'row'}, dimensions={1}, use_global_device_ids=true | all-gather | bytes 655360 | tf_op jit(solution)/shard_map/while/body/eval_jaxpr/all_gather | solution.py:77
  27.2 13.2 %all_to_all.17 = f32[8,8,2048]{2,0,1:T(8,128)S(1)} all-to-all(f32[8,8,2048]{2,0,1:T(8,128)S(1)} %bitcast.68), channel_id=1, replica_groups=mesh['tm'=8,'row'=4] {'tm'}, dimensions={1} | all-to-all | bytes 1048576 | tf_op jit(solution)/shard_map/while/body/eval_jaxpr/all_to_all | solution.py:78
  40.4 36.2 %fusion.36 = f32[64,4096]{1,0:T(8,128)} fusion(f32[4096,2048]{1,0:T(8,128)} %get-tuple-element.374, f32[8,8,2048]{2,0,1:T(8,128)S(1)} %all_to_all.17), kind=kOutput, calls=%fused_computation.clone.1 | convolution fusion | flops 6442450944 | bytes 35127296 | tf_op jit(solution)/shard_map/while/body/eval_jaxpr/dot_general | solution.py:49
  76.6 36.0 %reduce-scatter.2.cloned.1.call-done = f32[8,4096]{1,0:T(8,128)} async-done(((f32[64,4096]{1,0:T(8,128)}), f32[8,4096]{1,0:T(8,128)}) %reduce-scatter.2.cloned.1.call-update) | async-done | bytes 131088 | tf_op jit(solution)/shard_map/while/body/eval_jaxpr/reduce_scatter | solution.py:79
  113.7 15.4 %all_gather.8 = f32[8,16384]{1,0:T(8,128)S(1)} all-gather(f32[8,4096]{1,0:T(8,128)S(1)} %get-tuple-element.369), channel_id=1, replica_groups=mesh['tm'=8,'row'=4] {'row'}, dimensions={1}, use_global_device_ids=true | all-gather | bytes 655360 | tf_op jit(solution)/shard_map/while/body/eval_jaxpr/all_gather | solution.py:77
  129.0 12.3 %all_to_all.17 = f32[8,8,2048]{2,0,1:T(8,128)S(1)} all-to-all(f32[8,8,2048]{2,0,1:T(8,128)S(1)} %bitcast.68), channel_id=1, replica_groups=mesh['tm'=8,'row'=4] {'tm'}, dimensions={1} | all-to-all | bytes 1048576 | tf_op jit(solution)/shard_map/while/body/eval_jaxpr/all_to_all | solution.py:78
  141.3 36.2 %fusion.36 = f32[64,4096]{1,0:T(8,128)} fusion(f32[4096,2048]{1,0:T(8,128)} %get-tuple-element.374, f32[8,8,2048]{2,0,1:T(8,128)S(1)} %all_to_all.17), kind=kOutput, calls=%fused_computation.clone.1 | convolution fusion | flops 6442450944 | bytes 35127296 | tf_op jit(solution)/shard_map/while/body/eval_jaxpr/dot_general | solution.py:49
  177.5 36.0 %reduce-scatter.2.cloned.1.call-done = f32[8,4096]{1,0:T(8,128)} async-done(((f32[64,4096]{1,0:T(8,128)}), f32[8,4096]{1,0:T(8,128)}) %reduce-scatter.2.cloned.1.call-update) | async-done | bytes 131088 | tf_op jit(solution)/shard_map/while/body/eval_jaxpr/reduce_scatter | solution.py:79
  214.5 15.4 %all_gather.8 = f32[8,16384]{1,0:T(8,128)S(1)} all-gather(f32[8,4096]{1,0:T(8,128)S(1)} %get-tuple-element.369), channel_id=1, replica_groups=mesh['tm'=8,'row'=4] {'row'}, dimensions={1}, use_global_device_ids=true | all-gather | bytes 655360 | tf_op jit(solution)/shard_map/while/body/eval_jaxpr/all_gather | solution.py:77
  229.9 12.2 %all_to_all.17 = f32[8,8,2048]{2,0,1:T(8,128)S(1)} all-to-all(f32[8,8,2048]{2,0,1:T(8,128)S(1)} %bitcast.68), channel_id=1, replica_groups=mesh['tm'=8,'row'=4] {'tm'}, dimensions={1} | all-to-all | bytes 1048576 | tf_op jit(solution)/shard_map/while/body/eval_jaxpr/all_to_all | solution.py:78
  242.2 36.2 %fusion.36 = f32[64,4096]{1,0:T(8,128)} fusion(f32[4096,2048]{1,0:T(8,128)} %get-tuple-element.374, f32[8,8,2048]{2,0,1:T(8,128)S(1)} %all_to_all.17), kind=kOutput, calls=%fused_computation.clone.1 | convolution fusion | flops 6442450944 | bytes 35127296 | tf_op jit(solution)/shard_map/while/body/eval_jaxpr/dot_general | solution.py:49
  278.4 36.0 %reduce-scatter.2.cloned.1.call-done = f32[8,4096]{1,0:T(8,128)} async-done(((f32[64,4096]{1,0:T(8,128)}), f32[8,4096]{1,0:T(8,128)}) %reduce-scatter.2.cloned.1.call-update) | async-done | bytes 131088 | tf_op jit(solution)/shard_map/while/body/eval_jaxpr/reduce_scatter | solution.py:79
  315.4 15.4 %all_gather.8 = f32[8,16384]{1,0:T(8,128)S(1)} all-gather(f32[8,4096]{1,0:T(8,128)S(1)} %get-tuple-element.369), channel_id=1, replica_groups=mesh['tm'=8,'row'=4] {'row'}, dimensions={1}, use_global_device_ids=true | all-gather | bytes 655360 | tf_op jit(solution)/shard_map/while/body/eval_jaxpr/all_gather | solution.py:77
  330.8 12.3 %all_to_all.17 = f32[8,8,2048]{2,0,1:T(8,128)S(1)} all-to-all(f32[8,8,2048]{2,0,1:T(8,128)S(1)} %bitcast.68), channel_id=1, replica_groups=mesh['tm'=8,'row'=4] {'tm'}, dimensions={1} | all-to-all | bytes 1048576 | tf_op jit(solution)/shard_map/while/body/eval_jaxpr/all_to_all | solution.py:78
  343.0 36.2 %fusion.36 = f32[64,4096]{1,0:T(8,128)} fusion(f32[4096,2048]{1,0:T(8,128)} %get-tuple-element.374, f32[8,8,2048]{2,0,1:T(8,128)S(1)} %all_to_all.17), kind=kOutput, calls=%fused_computation.clone.1 | convolution fusion | flops 6442450944 | bytes 35127296 | tf_op jit(solution)/shard_map/while/body/eval_jaxpr/dot_general | solution.py:49
  379.2 36.0 %reduce-scatter.2.cloned.1.call-done = f32[8,4096]{1,0:T(8,128)} async-done(((f32[64,4096]{1,0:T(8,128)}), f32[8,4096]{1,0:T(8,128)}) %reduce-scatter.2.cloned.1.call-update) | async-done | bytes 131088 | tf_op jit(solution)/shard_map/while/body/eval_jaxpr/reduce_scatter | solution.py:79
  417.0 10.9 %fusion.16 = f32[256,256]{1,0:T(8,128)} fusion(f32[4096,256]{1,0:T(8,128)} %param.12, f32[4096,256]{1,0:T(8,128)} %param.13), kind=kOutput, calls=%fused_computation.29 | convolution fusion | flops 3221225472 | bytes 8650752 | tf_op jit(solution)/shard_map/dot_general | solution.py:45
  432.0 12.0 %psum.38 = f32[8,256]{1,0:T(8,128)S(1)} all-reduce(f32[8,256]{1,0:T(8,128)S(1)} %fusion.14), channel_id=1, replica_groups=mesh['tm'=8,'row'=4] {'row'}, use_global_device_ids=true, to_apply=%region_6.7 | all-reduce | flops 2048 | bytes 16384 | tf_op jit(solution)/shard_map/psum | solution.py:86
  454.4 18.3 %all-reduce.5.cloned.1.call-done = f32[8,4096]{1,0:T(8,128)} async-done(((f32[8,4096]{1,0:T(8,128)}), f32[8,4096]{1,0:T(8,128)}) %all-reduce.5.cloned.1.call-update) | async-done | bytes 131088 | tf_op jit(solution)/shard_map/psum | solution.py:14
  476.7 18.8 %all-reduce.1 = (f32[1,8,256]{2,1,0:T(8,128)S(1)}, f32[1,8,256]{2,1,0:T(8,128)S(1)}) all-reduce(f32[1,8,256]{2,1,0:T(8,128)S(1)} %convolution_bitcast_fusion.1, f32[1,8,256]{2,1,0:T(8,128)S(1)} %convolution_bitcast_fusion), channel_id=1, replica_groups=mesh['tm'=8,'row'=4] {'row'}, use_global_device_ids=true, to_apply=%region_1.2 | all-reduce | flops 4096 | bytes 32768 | tf_op jit(solution)/shard_map/psum | solution.py:89
  495.5 14.5 %all-reduce.7.cloned.1.call-done = f32[256,256]{1,0:T(8,128)} async-done(((f32[256,256]{1,0:T(8,128)}), f32[256,256]{1,0:T(8,128)}) %all-reduce.7.cloned.1.call-update) | async-done | bytes 262160 | tf_op jit(solution)/shard_map/psum | solution.py:89
  511.0 23.6 %all-gather.2.cloned.1.call-done = f32[8,8,4096]{2,1,0:T(8,128)} async-done(((f32[1,8,4096]{2,1,0:T(8,128)}), f32[8,8,4096]{2,1,0:T(8,128)}) %all-gather.2.cloned.1.call-update) | async-done | bytes 1048592 | tf_op jit(solution)/shard_map/all_gather | solution.py:19
  542.3 40.0 %while.41 = (s32[]{:T(128)}, f32[2,8,256]{2,1,0:T(8,128)S(1)}, f32[1,8,256]{2,1,0:T(8,128)S(1)}, s32[]{:T(128)}, f32[256,256]{1,0:T(8,128)S(1)}, /*index=5*/f32[1,8,256]{2,1,0:T(8,128)S(1)}, s32[]{:T(128)}, s32[]{:T(128)}) while((s32[]{:T(128)}, f32[2,8,256]{2,1,0:T(8,128)S(1)}, f32[1,8,256]{2,1,0:T(8,128)S(1)}, s32[]{:T(128)}, ...), condition=%wide.region_9.10_spmd.clone, body=%wide.region_8.9_spmd.clone.sunk | while | flops 6307844 | bytes 442514 | solution.py:110
  (84 shorter events, 87.9 us)
Async XLA Ops:
  9.8 102.8 %reduce-scatter.2.cloned.1.call-start = ((), (), s32[]{:S(2)}) async-start(), calls=%async_computation.5 | async-start | bytes 1179648 | tf_op jit(solution)/shard_map/while/body/eval_jaxpr/reduce_scatter | solution.py:79
  113.6 99.9 %reduce-scatter.2.cloned.1.call-start = ((), (), s32[]{:S(2)}) async-start(), calls=%async_computation.5 | async-start | bytes 1179648 | tf_op jit(solution)/shard_map/while/body/eval_jaxpr/reduce_scatter | solution.py:79
  214.5 99.9 %reduce-scatter.2.cloned.1.call-start = ((), (), s32[]{:S(2)}) async-start(), calls=%async_computation.5 | async-start | bytes 1179648 | tf_op jit(solution)/shard_map/while/body/eval_jaxpr/reduce_scatter | solution.py:79
  315.3 99.9 %reduce-scatter.2.cloned.1.call-start = ((), (), s32[]{:S(2)}) async-start(), calls=%async_computation.5 | async-start | bytes 1179648 | tf_op jit(solution)/shard_map/while/body/eval_jaxpr/reduce_scatter | solution.py:79
  416.2 56.5 %all-reduce.5.cloned.1.call-start = ((), (), s32[]{:S(2)}) async-start(), calls=%async_computation.2 | async-start | bytes 262144 | tf_op jit(solution)/shard_map/psum | solution.py:14
  416.8 11.2 %copy-start.1 = (f32[1,8,4096]{2,1,0:T(8,128)S(1)}, f32[1,8,4096]{2,1,0:T(8,128)}, u32[]{:S(2)}) copy-start(f32[1,8,4096]{2,1,0:T(8,128)} %param.10) | copy-start | bytes 393220
  416.8 93.2 %all-reduce.7.cloned.1.call-start = ((), (), s32[]{:S(2)}) async-start(), calls=%async_computation.3 | async-start | bytes 524288 | tf_op jit(solution)/shard_map/psum | solution.py:89
  428.0 106.6 %all-gather.2.cloned.1.call-start = ((), (), s32[]{:S(2)}) async-start(), calls=%async_computation.4 | async-start | bytes 1179648 | tf_op jit(solution)/shard_map/all_gather | solution.py:19
  454.4 127.9 %copy-start = (f32[1,8,4096]{2,1,0:T(8,128)S(1)}, f32[1,8,4096]{2,1,0:T(8,128)}, u32[]{:S(2)}) copy-start(f32[1,8,4096]{2,1,0:T(8,128)} %fusion.11) | copy-start | bytes 393220
  472.7 109.7 %copy-start.2 = (f32[8,4096]{1,0:T(8,128)S(1)}, f32[8,4096]{1,0:T(8,128)}, u32[]{:S(2)}) copy-start(f32[8,4096]{1,0:T(8,128)} %all-reduce.5.cloned.1.call-done) | copy-start | bytes 393220
  542.6 3.0 collective-permute-start
  545.8 4.1 collective-permute-start
  550.2 5.1 collective-permute-start
  555.5 5.1 collective-permute-start
  560.8 5.1 collective-permute-start
  566.1 5.1 collective-permute-start
  571.4 5.1 collective-permute-start
  576.7 5.6 collective-permute-start
Sparse Core Ops, SparseCore 0:
  76.8 35.8 reduce-scatter.1
  177.6 35.8 reduce-scatter.1
  278.5 35.8 reduce-scatter.1
  379.4 35.8 reduce-scatter.1
Sparse Core Ops, SparseCore 1:
  419.7 52.9 all-reduce.4
  474.9 35.1 all-reduce.6
  511.8 22.7 all-gather.1
where the time goes:
time: 605 us; the launch traced here: 596 us
  waiting for transfers between devices  208 us (34%)
  matrix products  182 us (30%)
  blocking collectives  144 us (24%)
  starting transfers between devices  31.8 us (5%)
  between operations  14.8 us (2%)
  other arithmetic  14.2 us (2%)
    dot_general x4, matrix products, times_columns(): lax.dot_general(vectors, operator, (((1,), (1,)), ((), ())), precision=hi...  145 us
    reduce_scatter x4, waiting for transfers between devices, fine_scatter(): lax.psum_scatter(times_columns(columns, operator), 'tm', scatter_dimensio...  144 us
    all_gather x4, blocking collectives, fine_scatter(): full_state = lax.all_gather(current, 'row', axis=1, tiled=True)  63.5 us
    all_to_all x4, blocking collectives, fine_scatter(): lax.all_to_all(full_state, 'tm', split_axis=1, concat_axis=0, tiled=True)  50 us
    ppermute x8, starting transfers between devices, shifted(): return lax.ppermute(block, axis, route)  31.3 us
    all_gather x1, waiting for transfers between devices, carried_in(): everything = lax.all_gather(array, axis)  23.6 us
    psum x1, blocking collectives, local(): lax.psum((project_rows(defects, coarse_right), matmul(coarse_left.T, coar...  18.8 us
    psum x1, waiting for transfers between devices, broadcast(): return lax.psum(jnp.where(mine, array, jnp.zeros_like(array)), axis)  18.3 us
  transfers between devices with their start and end apart: 15, of which 15 were waited for; matrix products, arithmetic and copies ran while one was open for 5% of the time, Pallas kernels for 0%

commit v1 on v0

v1 whole, which is shorter than its diff:
```python
import functools

import jax
import jax.numpy as jnp
from jax import lax
from jax.experimental import pallas as pl
from jax.experimental.pallas import tpu as pltpu
from jax.sharding import PartitionSpec as P

FINE = 4
MESH = pl.DeviceIdType.MESH

highest = lax.Precision.HIGHEST


def fine_kernel(
    T, R, fine_time,
    starts_ref, op_ref, first_ref, fine_ref,
    stage, pairs, arrivals, state, along, pieces, columns, half_send, half_recv, full_send, full_recv, own,
    load_sem, init_send, init_recv, z_send, z_recv, g_send, g_recv, h_send, h_recv, f_send, f_recv,
):
    t, r = lax.axis_index("tm"), lax.axis_index("row")
    E, rows = starts_ref.shape
    sub = rows // T
    S = T * E
    half = T // 2
    my_chip, my_core = t // 2, t % 2
    stage_rows = stage.shape[1]
    loads = rows // stage_rows

    def copy_to(src, dst, send, recv, tm, row):
        return pltpu.make_async_remote_copy(
            src_ref=src, dst_ref=dst, send_sem=send, recv_sem=recv, device_id=(tm, row), device_id_type=MESH
        )

    def load(k):
        slot = k % 2
        return pltpu.make_async_copy(
            op_ref.at[pl.ds(k * stage_rows, stage_rows)], stage.at[slot], load_sem.at[slot]
        )

    def init_copy(d):
        dest = lax.rem(t + d, T)
        src = starts_ref.at[:, pl.ds(pl.multiple_of(dest * sub, sub), sub)]
        return copy_to(src, arrivals.at[t], init_send.at[dest], init_recv.at[t], dest, r)

    for d in range(1, T):
        init_copy(d).start()
    load(0).start()
    load(1).start()

    def convert(k, unused):
        load(k).wait()
        base = pl.multiple_of(k * stage_rows, stage_rows)
        for c in range(R):
            x = stage[k % 2, :, c * sub : (c + 1) * sub]
            high = x.astype(jnp.bfloat16)
            low = (x - high.astype(jnp.float32)).astype(jnp.bfloat16)
            pairs[pl.ds(base, stage_rows), 2 * c * sub : (2 * c + 1) * sub] = high
            pairs[pl.ds(base, stage_rows), (2 * c + 1) * sub : (2 * c + 2) * sub] = low

        @pl.when(k + 2 < loads)
        def _():
            load(k + 2).start()

        return unused

    quarter = max(loads // 4, 1)
    bounds = [0, quarter, loads]

    lax.fori_loop(bounds[0], bounds[1], convert, 0)
    arrivals[t] = starts_ref[:, pl.ds(pl.multiple_of(t * sub, sub), sub)]
    for d in range(1, T):
        source = lax.rem(t + T - d, T)
        copy_to(arrivals.at[source], arrivals.at[source], init_send.at[source], init_recv.at[source], source, r).wait_recv()
    for k in range(T):
        state[k * E : (k + 1) * E, :] = arrivals[k]
        first_ref[k * E : (k + 1) * E, :] = arrivals[k]

    def step(i, filler):
        def z_copy(d):
            dest = lax.rem(r + d, R)
            return copy_to(state, along.at[i, r], z_send.at[dest], z_recv.at[i, r], t, dest)

        order = [d for d in range(1, R)]
        for d in order:
            z_copy(d).start()
        if filler is not None:
            filler()

        def piece_copy(source_row, block):
            index = source_row * T + t
            dest = index // R
            place = lax.rem(index, R)
            return dest, place, copy_to(
                block, pieces.at[i, place], g_send.at[source_row], g_recv.at[i, place], dest, r
            )

        def forward(source_row, block):
            dest, place, copy = piece_copy(source_row, block)

            @pl.when(dest != t)
            def _():
                copy.start()

            @pl.when(dest == t)
            def _():
                pieces[i, place] = block[...]

        forward(r, state)
        for d in order:
            source_row = lax.rem(r + R - d, R)
            copy_to(along.at[i, source_row], along.at[i, source_row], z_send.at[source_row], z_recv.at[i, source_row], t, source_row).wait_recv()
            forward(source_row, along.at[i, source_row])

        for j in range(R):
            source = lax.rem(t * R + j, T)

            @pl.when(source != t)
            def _():
                copy_to(pieces.at[i, j], pieces.at[i, j], g_send.at[j], g_recv.at[i, j], source, r).wait_recv()

            x = pieces[i, j]
            high = x.astype(jnp.bfloat16).astype(jnp.float32)
            both = jnp.concatenate([high, x - high], axis=0)
            turned = both.T.astype(jnp.bfloat16)
            columns[2 * j * sub : (2 * j + 1) * sub, :] = turned
            columns[(2 * j + 1) * sub : (2 * j + 2) * sub, :] = turned

        def image(target):
            base = pl.multiple_of(target * sub, sub)
            out = jnp.dot(pairs[pl.ds(base, sub), :], columns[...], preferred_element_type=jnp.float32)
            out = out.T
            return out[:S] + out[S:]

        def chip_at(k):
            return lax.rem(my_chip + 1 + k, half)

        def half_copy(q):
            return copy_to(half_send.at[q], half_recv.at[i, q], h_send.at[q], h_recv.at[i, q], t + 1 - 2 * my_core, r)

        def full_copy(q):
            return copy_to(full_send.at[q], full_recv.at[i, my_chip], f_send.at[q], f_recv.at[i, my_chip], 2 * q + my_core, r)

        def for_partner(k, unused):
            q = chip_at(k)
            half_send[q] = image(2 * q + 1 - my_core)
            half_copy(q).start()
            return unused

        lax.fori_loop(0, half, for_partner, 0)

        def for_others(k, unused):
            q = chip_at(k)
            mine = image(2 * q + my_core)
            half_copy(q).wait_recv()
            both = mine + half_recv[i, q]

            @pl.when(k < half - 1)
            def _():
                full_send[q] = both
                full_copy(q).start()

            @pl.when(k == half - 1)
            def _():
                own[...] = both

            return unused

        lax.fori_loop(0, half, for_others, 0)

        for d in order:
            z_copy(d).wait_send()
        for row in range(R):
            dest, unused_place, copy = piece_copy(jnp.int32(row), state)

            @pl.when(dest != t)
            def _():
                copy.wait_send()

        total = own[...]
        for k in range(half - 1):
            q = lax.rem(my_chip + half - 1 - k, half)
            copy_to(full_recv.at[i, q], full_recv.at[i, q], f_send.at[q], f_recv.at[i, q], 2 * q + my_core, r).wait_recv()
            total = total + full_recv[i, q]
        state[...] = state[...] + fine_time * total
        for q in range(half):
            half_copy(q).wait_send()

            @pl.when(q != my_chip)
            def _():
                full_copy(q).wait_send()

    def rest():
        lax.fori_loop(bounds[1], bounds[2], convert, 0)

    step(0, rest)
    for d in range(1, T):
        init_copy(d).wait_send()

    def later(i, unused):
        step(i, None)
        return unused

    lax.fori_loop(1, FINE, later, 0)
    fine_ref[...] = state[...]


def fine_steps(starts, operator, T, R, fine_time):
    E, rows = starts.shape
    columns = operator.shape[1]
    sub = rows // T
    S = T * E
    half = T // 2
    stage_rows = min(256, rows // 8)
    f32, bf16 = jnp.float32, jnp.bfloat16
    dma = pltpu.SemaphoreType.DMA
    vmem = pl.BlockSpec(memory_space=pltpu.VMEM)
    return pl.pallas_call(
        functools.partial(fine_kernel, T, R, fine_time),
        out_shape=[jax.ShapeDtypeStruct((S, sub), f32)] * 2,
        in_specs=[vmem, pl.BlockSpec(memory_space=pl.ANY)],
        out_specs=[vmem, vmem],
        scratch_shapes=[
            pltpu.VMEM((2, stage_rows, columns), f32),
            pltpu.VMEM((rows, 2 * columns), bf16),
            pltpu.VMEM((T, E, sub), f32),
            pltpu.VMEM((S, sub), f32),
            pltpu.VMEM((FINE, R, S, sub), f32),
            pltpu.VMEM((FINE, R, S, sub), f32),
            pltpu.VMEM((2 * columns, 2 * S), bf16),
            pltpu.VMEM((half, S, sub), f32),
            pltpu.VMEM((FINE, half, S, sub), f32),
            pltpu.VMEM((half, S, sub), f32),
            pltpu.VMEM((FINE, half, S, sub), f32),
            pltpu.VMEM((S, sub), f32),
            dma((2,)),
            dma((T,)),
            dma((T,)),
            dma((R,)),
            dma((FINE, R)),
            dma((R,)),
            dma((FINE, R)),
            dma((half,)),
            dma((FINE, half)),
            dma((half,)),
            dma((FINE, half)),
        ],
        compiler_params=pltpu.CompilerParams(has_side_effects=True, vmem_limit_bytes=60 * 2**20),
    )(starts, operator)


def local(starts, operator, coarse_left, coarse_right):
    T, R = lax.axis_size("tm"), lax.axis_size("row")
    t = lax.axis_index("tm")
    E, rows = starts.shape[1:]
    sub = rows // T
    rank = coarse_right.shape[1]
    step_time = 1.0 / T
    cross = lax.psum(jnp.dot(coarse_left.T, coarse_right, precision=highest), "row")
    first, fine = fine_steps(starts[0], operator, T, R, step_time / FINE)
    right = lax.dynamic_slice_in_dim(coarse_right, t * sub, sub, 0)
    both = jnp.concatenate([first, fine], axis=0)
    projected = lax.psum(jnp.dot(both, right, precision=highest), ("tm", "row"))
    old = projected[: T * E].reshape(T, E, rank)
    new = projected[T * E :].reshape(T, E, rank)
    first, fine = first.reshape(T, E, sub), fine.reshape(T, E, sub)
    sums = first[:1] + jnp.cumsum(fine - first, axis=0)
    sums = lax.all_to_all(sums, "tm", split_axis=0, concat_axis=2, tiled=True)
    kernel = jnp.eye(rank, dtype=jnp.float32) + step_time * cross
    w = jnp.zeros((E, rank), jnp.float32)
    total = w
    mine = w
    for m in range(T - 1):
        w = jnp.dot(w, kernel, precision=highest) + new[m] - old[m + 1]
        total = total + w
        mine = jnp.where(t == m + 1, total, mine)
    spread = lax.dot_general(mine, coarse_left, (((1,), (1,)), ((), ())), precision=highest)
    return sums + (step_time * spread)[None]


def solution(mesh):
    in_specs = (P("tm", None, "row"), P("row", "tm"), P("row", None), P("row", None))
    out_specs = P("tm", None, "row")
    return jax.shard_map(local, mesh=mesh, in_specs=in_specs, out_specs=out_specs, check_vma=False)
```

time: 605 us -> 337 us (0.56); the launches traced: 596 us -> 336 us
  matrix products: 182 us -> 28 us
  blocking collectives: 144 us -> 0 us
  Pallas kernels: 0 us -> 142 us
  waiting for transfers between devices: 208 us -> 148 us
  starting transfers between devices: 31.8 us -> 3.89 us
  other arithmetic: 14.2 us -> 0.68 us
    dot_general x18 -> x10, matrix products: 182 us -> 28 us  [the longest x1 10.9 us: local(): jnp.dot(coarse_left.T, coarse_right, precision=highest)]
    reduce_scatter x4 -> x0, waiting for transfers between devices: 144 us -> none  [fine_scatter(): lax.psum_scatter(times_columns(columns, operator), 'tm', scatter_dimensio...]
    pallas_call x0 -> x1, Pallas kernels: none -> 142 us  [fine_steps(): pl.pallas_call(functools.partial(fine_kernel, T, R, fine_time), out_shape...]
    psum x2, waiting for transfers between devices: 32.8 us -> 148 us  [the longest x1 111 us: local(): projected = lax.psum(jnp.dot(both, right, precision=highest), ('tm', 'row'))]
    all_gather x4 -> x0, blocking collectives: 63.5 us -> none  [fine_scatter(): full_state = lax.all_gather(current, 'row', axis=1, tiled=True)]
    all_to_all x4 -> x0, blocking collectives: 50 us -> none  [fine_scatter(): lax.all_to_all(full_state, 'tm', split_axis=1, concat_axis=0, tiled=True)]
    ppermute x8 -> x0, starting transfers between devices: 31.3 us -> none  [shifted(): return lax.ppermute(block, axis, route)]
    psum x2 -> x0, blocking collectives: 30.8 us -> none  [the longest x1 18.8 us: local(): lax.psum((project_rows(defects, coarse_right), matmul(coarse_left.T, coar...]
  transfers between devices with their start and end apart: 15 -> 3, of which waited for: 15 -> 2; matrix products, arithmetic and copies ran while one was open for 5% -> 6% of each run, Pallas kernels for 0% -> 0%
where the time goes in v1:
time: 337 us; the launch traced here: 336 us
  waiting for transfers between devices  148 us (44%)
  Pallas kernels  142 us (42%)
  matrix products  28 us (8%)
  between operations  13.5 us (4%)
  starting transfers between devices  3.89 us (1%)
    pallas_call x1, Pallas kernels, fine_steps(): pl.pallas_call(functools.partial(fine_kernel, T, R, fine_time), out_shape...  142 us
    psum x1, waiting for transfers between devices, local(): projected = lax.psum(jnp.dot(both, right, precision=highest), ('tm', 'row'))  111 us
    psum x1, waiting for transfers between devices, local(): lax.psum(jnp.dot(coarse_left.T, coarse_right, precision=highest), 'row')  37 us
    dot_general x1, matrix products, local(): jnp.dot(coarse_left.T, coarse_right, precision=highest)  10.9 us
    dot_general x7, matrix products, local(): w = jnp.dot(w, kernel, precision=highest) + new[m] - old[m + 1]  8.5 us
  transfers between devices with their start and end apart: 3, of which 2 were waited for; matrix products, arithmetic and copies ran while one was open for 6% of the time, Pallas kernels for 0%

profile of v1, /device:TPU:0, one launch (start us, length us, event | category | flops | bytes accessed | tf_op | source)
XLA Modules:
  0.0 336.4 jit_solution(17212371663609977496)
XLA Ops:
  6.5 0.0 all-reduce.5.cloned.1.call-start
  6.5 141.8 %shard_map.46 = (f32[64,512]{1,0:T(8,128)}, f32[64,512]{1,0:T(8,128)}) custom-call(f32[8,4096]{1,0:T(8,128)} %bitcast.22, f32[4096,2048]{1,0:T(8,128)} %op_ref.1), custom_call_target="tpu_custom_call" | custom-call | tf_op jit(solution)/shard_map/pallas_call | solution.py:219
  148.4 2.3 fusion.11
  150.6 0.0 all-reduce.5.cloned.1.call-update
  150.7 0.0 copy-start
  150.7 0.0 copy-start.1
  150.7 0.2 all-reduce.3.cloned.1.call-start
  150.9 10.9 %fusion.22 = f32[256,256]{1,0:T(8,128)} fusion(f32[4096,256]{1,0:T(8,128)} %param.6, f32[4096,256]{1,0:T(8,128)} %param.7), kind=kOutput, calls=%fused_computation.33 | convolution fusion | flops 3221225472 | bytes 8650752 | tf_op jit(solution)/shard_map/dot_general | solution.py:260
  161.8 0.0 all-reduce.3.cloned.1.call-update
  161.9 0.0 copy-done
  161.9 0.0 copy-done.1
  161.9 0.7 reduce-window_add_fusion
  162.6 3.7 %all-to-all-start = ((f32[8,8,512]{2,1,0:T(8,128)}), f32[8,8,512]{2,1,0:T(8,128)S(1)}, u32[]{:S(2)}, u32[]{:S(2)}) async-start(f32[8,8,512]{2,1,0:T(8,128)} %reduce-window_add_fusion), calls=%async_computation | async-start | bytes 262144 | tf_op jit(solution)/shard_map/all_to_all | solution.py:269
  166.2 111.4 %all-reduce.5.cloned.1.call-done = f32[128,256]{1,0:T(8,128)} async-done(((f32[128,256]{1,0:T(8,128)}), f32[128,256]{1,0:T(8,128)}) %all-reduce.5.cloned.1.call-update) | async-done | bytes 131088 | tf_op jit(solution)/shard_map/psum | solution.py:264
  277.7 37.0 %all-reduce.3.cloned.1.call-done = f32[256,256]{1,0:T(8,128)} async-done(((f32[256,256]{1,0:T(8,128)}), f32[256,256]{1,0:T(8,128)}) %all-reduce.3.cloned.1.call-update) | async-done | bytes 262160 | tf_op jit(solution)/shard_map/psum | solution.py:260
  314.7 1.2 fusion.10
  315.9 1.2 fusion.9
  317.1 1.2 fusion.8
  318.3 1.2 fusion.7
  319.5 1.2 fusion.6
  320.7 1.2 fusion.5
  322.0 1.2 fusion.4
  323.2 0.0 all-to-all-done
  323.2 6.3 %fusion.1 = f32[1,8,4096]{2,1,0:T(8,128)} fusion(f32[8,4096]{1,0:T(8,128)S(1)} %bitcast.21, f32[8,256]{1,0:T(8,128)S(1)} %fusion.4, f32[4096,256]{1,0:T(8,128)} %param.6), kind=kOutput, calls=%fused_computation.2 | convolution fusion | flops 100728832 | bytes 4464640 | tf_op jit(solution)/shard_map/dot_general | solution.py:278
  (1 shorter events, 0.0 us)
Async XLA Ops:
  6.5 271.1 %all-reduce.5.cloned.1.call-start = ((), (), s32[]{:S(2)}) async-start(), calls=%async_computation.2 | async-start | bytes 262144 | tf_op jit(solution)/shard_map/psum | solution.py:264
  150.7 11.2 %copy-start = (f32[64,512]{1,0:T(8,128)S(1)}, f32[64,512]{1,0:T(8,128)}, u32[]{:S(2)}) copy-start(f32[64,512]{1,0:T(8,128)} %get-tuple-element.7) | copy-start | bytes 393220
  150.7 11.2 %copy-start.1 = (f32[64,512]{1,0:T(8,128)S(1)}, f32[64,512]{1,0:T(8,128)}, u32[]{:S(2)}) copy-start(f32[64,512]{1,0:T(8,128)} %get-tuple-element.8) | copy-start | bytes 393220
  150.7 164.0 %all-reduce.3.cloned.1.call-start = ((), (), s32[]{:S(2)}) async-start(), calls=%async_computation.1 | async-start | bytes 524288 | tf_op jit(solution)/shard_map/psum | solution.py:260
  162.6 160.7 %all-to-all-start = ((f32[8,8,512]{2,1,0:T(8,128)}), f32[8,8,512]{2,1,0:T(8,128)S(1)}, u32[]{:S(2)}, u32[]{:S(2)}) async-start(f32[8,8,512]{2,1,0:T(8,128)} %reduce-window_add_fusion), calls=%async_computation | async-start | bytes 262144 | tf_op jit(solution)/shard_map/all_to_all | solution.py:269
Sparse Core Ops, SparseCore 0:
  150.8 126.8 all-reduce.4
  280.0 34.6 all-reduce.2

commit v2 on v1

--- a/solution.py
+++ b/solution.py
@@ -257,11 +257,18 @@
     sub = rows // T
     rank = coarse_right.shape[1]
     step_time = 1.0 / T
-    cross = lax.psum(jnp.dot(coarse_left.T, coarse_right, precision=highest), "row")
     first, fine = fine_steps(starts[0], operator, T, R, step_time / FINE)
     right = lax.dynamic_slice_in_dim(coarse_right, t * sub, sub, 0)
     both = jnp.concatenate([first, fine], axis=0)
-    projected = lax.psum(jnp.dot(both, right, precision=highest), ("tm", "row"))
+    width = rank // T
+    left = lax.dynamic_slice_in_dim(coarse_left, t * width, width, 1)
+    cross_part = lax.dot_general(left, coarse_right, (((0,), (0,)), ((), ())), precision=highest)
+    part = jnp.dot(both, right, precision=highest).reshape(T, 2 * E, rank)
+    part = jnp.sum(lax.all_to_all(part, "tm", split_axis=0, concat_axis=0, tiled=True), axis=0)
+    part = jnp.sum(lax.all_gather(jnp.concatenate([part, cross_part], axis=0), "row"), axis=0)
+    parts = lax.all_gather(part, "tm")
+    projected = parts[:, : 2 * E].reshape(2 * T * E, rank)
+    cross = parts[:, 2 * E :].reshape(rank, rank)
     old = projected[: T * E].reshape(T, E, rank)
     new = projected[T * E :].reshape(T, E, rank)
     first, fine = first.reshape(T, E, sub), fine.reshape(T, E, sub)

time: 337 us -> 194 us (0.58)
  waiting for transfers between devices: 148 us -> 0.01 us
  blocking collectives: 0 us -> 25 us
  between operations: 13.5 us -> 0.13 us
  matrix products: 28 us -> 17.2 us
  starting transfers between devices: 3.89 us -> 7.88 us
    psum x2 -> x0, waiting for transfers between devices: 148 us -> none  [the longest x1 111 us: local(): projected = lax.psum(jnp.dot(both, right, precision=highest), ('tm', 'row'))]
    all_gather x0 -> x2, blocking collectives: none -> 25 us  [the longest x1 14.9 us: local(): lax.all_gather(jnp.concatenate([part, cross_part], axis=0), 'row')]
    dot_general x7, matrix products: 8.5 us -> 1.57 us  [local(): w = jnp.dot(w, kernel, precision=highest) + new[m] - old[m + 1]]
    dot_general x2, matrix products: 13.2 us -> 9.28 us  [the longest x1 7 us: local(): lax.dot_general(left, coarse_right, (((0,), (0,)), ((), ())), precision=h...]
    all_to_all x0 -> x1, starting transfers between devices: none -> 3.68 us  [local(): lax.all_to_all(part, 'tm', split_axis=0, concat_axis=0, tiled=True)]
  transfers between devices with their start and end apart: 3 -> 2, of which waited for: 2 -> 0; matrix products, arithmetic and copies ran while one was open for 6% -> 5% of each run, Pallas kernels for 0% -> 0%
where the time goes in v2:
time: 194 us; the launch traced here: 193 us
  Pallas kernels  142 us (73%)
  blocking collectives  25 us (13%)
  matrix products  17.2 us (9%)
  starting transfers between devices  7.88 us (4%)
    pallas_call x1, Pallas kernels, fine_steps(): pl.pallas_call(functools.partial(fine_kernel, T, R, fine_time), out_shape...  142 us
    all_gather x1, blocking collectives, local(): lax.all_gather(jnp.concatenate([part, cross_part], axis=0), 'row')  14.9 us
    all_gather x1, blocking collectives, local(): parts = lax.all_gather(part, 'tm')  10.1 us
    dot_general x1, matrix products, local(): lax.dot_general(left, coarse_right, (((0,), (0,)), ((), ())), precision=h...  7 us
    dot_general x1, matrix products, local(): lax.dot_general(mine, coarse_left, (((1,), (1,)), ((), ())), precision=hi...  6.31 us
    all_to_all x1, starting transfers between devices, local(): sums = lax.all_to_all(sums, 'tm', split_axis=0, concat_axis=2, tiled=True)  4.2 us
  transfers between devices with their start and end apart: 2, of which 0 were waited for; matrix products, arithmetic and copies ran while one was open for 5% of the time, Pallas kernels for 0%

profile of v2, /device:TPU:0, one launch (start us, length us, event | category | flops | bytes accessed | tf_op | source)
XLA Modules:
  0.0 193.5 jit_solution(13237021991985824324)
XLA Ops:
  0.0 141.8 %shard_map.46 = (f32[64,512]{1,0:T(8,128)}, f32[64,512]{1,0:T(8,128)}) custom-call(f32[8,4096]{1,0:T(8,128)} %bitcast.108, f32[4096,2048]{1,0:T(8,128)} %op_ref.1), custom_call_target="tpu_custom_call" | custom-call | tf_op jit(solution)/shard_map/pallas_call | solution.py:219
  141.8 0.0 copy-start
  141.9 0.0 copy-start.1
  141.9 2.3 %fusion.13 = f32[128,256]{1,0:T(8,128)} fusion(f32[4096,256]{1,0:T(8,128)} %param.7, s32[]{:T(128)S(6)} %select_n.51, f32[64,512]{1,0:T(8,128)} %get-tuple-element.8, f32[64,512]{1,0:T(8,128)} %get-tuple-element.7), kind=kOutput, calls=%fused_computation.22 | convolution fusion | flops 201392128 | bytes 917508 | tf_op jit(solution)/shard_map/dot_general | solution.py:266
  144.1 3.7 %all-to-all-start.1 = ((f32[8,16,256]{2,1,0:T(8,128)}), f32[8,16,256]{2,1,0:T(8,128)S(1)}, u32[]{:S(2)}, u32[]{:S(2)}) async-start(f32[8,16,256]{2,1,0:T(8,128)} %bitcast.5), calls=%async_computation.1 | async-start | bytes 262144 | tf_op jit(solution)/shard_map/all_to_all | solution.py:267
  147.8 0.7 slice.60
  148.5 7.0 %fusion.2 = f32[32,256]{1,0:T(8,128)S(1)} fusion(f32[4096,256]{1,0:T(8,128)} %param.7, f32[4096,256]{1,0:T(8,128)} %param.6, s32[]{:T(128)S(6)} %select_n.52), kind=kOutput, calls=%fused_computation.3 | convolution fusion | flops 402653184 | bytes 6324228 | tf_op jit(solution)/shard_map/dot_general | solution.py:265
  155.6 0.0 copy-done
  155.6 0.0 copy-done.1
  155.6 0.7 reduce-window_add_fusion
  156.2 0.0 all-to-all-done.1
  156.3 4.2 %all-to-all-start = ((f32[8,8,512]{2,1,0:T(8,128)}), f32[8,8,512]{2,1,0:T(8,128)S(1)}, u32[]{:S(2)}, u32[]{:S(2)}) async-start(f32[8,8,512]{2,1,0:T(8,128)} %reduce-window_add_fusion), calls=%async_computation | async-start | bytes 262144 | tf_op jit(solution)/shard_map/all_to_all | solution.py:276
  160.5 14.9 %all-gather = f32[192,256]{1,0:T(8,128)S(1)} all-gather(f32[48,256]{1,0:T(8,128)S(1)} %pad_maximum_fusion), channel_id=2, replica_groups=mesh['tm'=8,'row'=4] {'row'}, dimensions={0}, use_global_device_ids=true | all-gather | bytes 245760 | tf_op jit(solution)/shard_map/all_gather | solution.py:268
  175.4 10.1 %all-gather.1 = f32[384,256]{1,0:T(8,128)S(1)} all-gather(f32[48,256]{1,0:T(8,128)S(1)} %reduce_sum.19), channel_id=3, replica_groups=mesh['tm'=8,'row'=4] {'tm'}, dimensions={0}, use_global_device_ids=true | all-gather | bytes 442368 | tf_op jit(solution)/shard_map/all_gather | solution.py:269
  185.5 0.2 fusion.12
  185.7 0.2 fusion.11
  186.0 0.2 fusion.10
  186.2 0.2 fusion.9
  186.4 0.2 fusion.8
  186.6 0.2 fusion.7
  186.9 0.2 fusion.6
  187.1 0.0 all-to-all-done
  187.2 6.3 %fusion.1 = f32[1,8,4096]{2,1,0:T(8,128)} fusion(f32[8,4096]{1,0:T(8,128)S(1)} %bitcast.93, f32[8,256]{1,0:T(8,128)S(1)} %fusion.6, f32[4096,256]{1,0:T(8,128)} %param.6), kind=kOutput, calls=%fused_computation.2 | convolution fusion | flops 100728832 | bytes 4464640 | tf_op jit(solution)/shard_map/dot_general | solution.py:285
  (6 shorter events, 0.1 us)
Async XLA Ops:
  141.8 13.7 %copy-start = (f32[64,512]{1,0:T(8,128)S(1)}, f32[64,512]{1,0:T(8,128)}, u32[]{:S(2)}) copy-start(f32[64,512]{1,0:T(8,128)} %get-tuple-element.7) | copy-start | bytes 393220
  141.9 13.7 %copy-start.1 = (f32[64,512]{1,0:T(8,128)S(1)}, f32[64,512]{1,0:T(8,128)}, u32[]{:S(2)}) copy-start(f32[64,512]{1,0:T(8,128)} %get-tuple-element.8) | copy-start | bytes 393220
  144.1 12.1 %all-to-all-start.1 = ((f32[8,16,256]{2,1,0:T(8,128)}), f32[8,16,256]{2,1,0:T(8,128)S(1)}, u32[]{:S(2)}, u32[]{:S(2)}) async-start(f32[8,16,256]{2,1,0:T(8,128)} %bitcast.5), calls=%async_computation.1 | async-start | bytes 262144 | tf_op jit(solution)/shard_map/all_to_all | solution.py:267
  156.3 30.9 %all-to-all-start = ((f32[8,8,512]{2,1,0:T(8,128)}), f32[8,8,512]{2,1,0:T(8,128)S(1)}, u32[]{:S(2)}, u32[]{:S(2)}) async-start(f32[8,8,512]{2,1,0:T(8,128)} %reduce-window_add_fusion), calls=%async_computation | async-start | bytes 262144 | tf_op jit(solution)/shard_map/all_to_all | solution.py:276
